TPU v7x, 32 devices: a whole 2x2x4 slice. The times are simulated.
32 devices in a mesh: tm: 32 (over z, y, x, core), prod: 1.
Axes of the slice: x: 2, y: 2, z: 4, core: 2. Of those that a mesh axis runs over, the one named last changes fastest.
Arguments:
- sales_records: float32 [1024, 16, 16, 128], P('tm', 'prod'), may hold values from -6 to 6
- day_month: int32 [1024], replicated, may hold values from 0 to 31, as said below
- month_year: int32 [32], replicated, may hold values from 0 to 3, never falling along the last dimension, each value on 1 to 16 neighbouring positions
- product_category: int32 [16], replicated, may hold values from 0 to 31
- store_region: int32 [16], replicated, may hold values from 0 to 3
Outputs:
- month_detail: float32 [32, 32, 4, 128], P('tm', 'prod')
- month_category: float32 [32, 32, 128], P('tm', 'prod')
- month_region: float32 [32, 4, 128], P('tm')
- month_totals: float32 [32, 128], P('tm')
- year_detail: float32 [4, 32, 4, 128], replicated
- year_category: float32 [4, 32, 128], replicated
- year_region: float32 [4, 4, 128], replicated
- year_totals: float32 [4, 128], replicated
Inputs may be any that keep to these rules, and one draw needn't show every extreme that they name: `day_month`: never falls along the days; month m, for m of 1 to 31, begins at a day from m * 32 - 31 // 2 to m * 32 + 31 // 2, and both ends of that range are taken in every draw. `month_year`: never falls along the months; every year has 1 to 16 months, one exactly that many.
All inputs are finite; a program needn't handle non-finite values.
Results may differ from a plain program's by a relative error of at most 0.0001.
Values sent between devices are 32-bit elements; how exact they have to be, the bound alone decides.
No kernel may reach another device: no remote copies, remote signals or barrier semaphores. Data moves between devices by JAX's collectives and lax.ppermute only.
A program may use at most 64 MiB of HBM per device.

v0:
```python
import jax
import jax.numpy as jnp
from jax import lax
from jax.sharding import PartitionSpec as P

MON_DEV = 1
CATEGORY_COUNT = 32
REGION_COUNT = 4


def with_halo(block, sides, width):
    for axis, dim in sides:
        count = lax.axis_size(axis)
        forward = [(i, i + 1) for i in range(count - 1)]
        backward = [(target, source) for source, target in forward]
        low = lax.ppermute(
            lax.slice_in_dim(block, block.shape[dim] - width, None, axis=dim), axis, forward
        )
        high = lax.ppermute(lax.slice_in_dim(block, 0, width, axis=dim), axis, backward)
        block = jnp.concatenate([low, block, high], axis=dim)
    return block


def onehot(labels, width):
    return (labels[:, None] == jnp.arange(width, dtype=jnp.int32)[None, :]).astype(jnp.float32)


def scaled(sums, counts):
    return sums / jnp.sqrt(counts)


def shards(sales_records, day_month, month_year, product_category, store_region):
    highest = lax.Precision.HIGHEST
    day_dev = sales_records.shape[0]
    prod_dev = sales_records.shape[1]
    stores = float(sales_records.shape[2])
    month_width = month_year.shape[0]
    year_width = max(month_width // 8, 2)
    cats_dev = CATEGORY_COUNT // lax.axis_size("prod")
    products = float(prod_dev * lax.axis_size("prod"))
    time_index = lax.axis_index("tm")
    prod_index = lax.axis_index("prod")
    month_hot = onehot(day_month, month_width)
    year_hot = onehot(month_year, year_width)
    category_hot = onehot(product_category, CATEGORY_COUNT)
    region_hot = onehot(store_region, REGION_COUNT)
    local_products = lax.dynamic_slice_in_dim(category_hot, prod_index * prod_dev, prod_dev, 0)
    by_region = jnp.einsum("dpsq,sr->dprq", sales_records, region_hot, precision=highest)
    by_category = jnp.einsum("dprq,pc->dcrq", by_region, local_products, precision=highest)
    month_days = jnp.sum(month_hot, 0)
    year_days = jnp.dot(month_days, year_hot, precision=highest)
    category_size = jnp.sum(category_hot, 0)
    region_size = jnp.sum(region_hot, 0)
    own_days = lax.dynamic_slice_in_dim(month_days, time_index * MON_DEV, MON_DEV, 0)
    own_sizes = lax.dynamic_slice_in_dim(category_size, prod_index * cats_dev, cats_dev, 0)
    local_labels = lax.dynamic_slice_in_dim(day_month, time_index * day_dev, day_dev, 0)
    window_ids = time_index - 1 + jnp.arange(3, dtype=jnp.int32)
    window_hot = (local_labels[:, None] == window_ids[None, :]).astype(jnp.float32)
    partial_value = jnp.einsum("dcrq,dk->kcrq", by_category, window_hot, precision=highest)
    clipped = jnp.clip(window_ids, 0, month_width - 1)
    inside = ((window_ids >= 0) & (window_ids < month_width)).astype(jnp.float32)
    source_years = onehot(month_year[clipped], year_width) * inside[:, None]
    padded = with_halo(partial_value, (("tm", 0),), 1)
    summed = padded[0:1] + padded[2:3] + padded[4:5]
    detail = lax.psum_scatter(summed, "prod", scatter_dimension=1, tiled=True)
    year_part = jnp.einsum("mcrq,my->ycrq", partial_value, source_years, precision=highest)
    year_cube = lax.psum(year_part, ("tm", "prod"))
    cell = own_days[:, None, None] * own_sizes[None, :, None] * region_size[None, None, :]
    month_detail = scaled(detail, jnp.maximum(cell, 1.0)[..., None])
    month_cat = jnp.sum(detail, 2)
    month_category = scaled(
        month_cat, jnp.maximum(own_days[:, None] * own_sizes[None, :] * stores, 1.0)[..., None]
    )
    month_reg = lax.psum(jnp.sum(detail, 1), "prod")
    month_region = scaled(
        month_reg, jnp.maximum(own_days[:, None] * products * region_size[None, :], 1.0)[..., None]
    )
    month_totals = scaled(jnp.sum(month_reg, 1), (own_days * products * stores)[:, None])
    year_cell = year_days[:, None, None] * category_size[None, :, None] * region_size[None, None, :]
    year_detail = scaled(year_cube, jnp.maximum(year_cell, 1.0)[..., None])
    year_cat = jnp.sum(year_cube, 2)
    year_category = scaled(
        year_cat, jnp.maximum(year_days[:, None] * category_size[None, :] * stores, 1.0)[..., None]
    )
    year_reg = jnp.sum(year_cube, 1)
    year_region = scaled(
        year_reg, jnp.maximum(year_days[:, None] * products * region_size[None, :], 1.0)[..., None]
    )
    year_totals = scaled(jnp.sum(year_reg, 1), (year_days * products * stores)[:, None])
    return (
        month_detail,
        month_category,
        month_region,
        month_totals,
        year_detail,
        year_category,
        year_region,
        year_totals,
    )


def solution(mesh):
    placed = (P("tm", "prod", None, None), P(), P(), P(), P())
    return jax.shard_map(
        shards,
        mesh=mesh,
        in_specs=placed,
        out_specs=(
            P("tm", "prod", None, None),
            P("tm", "prod", None),
            P("tm", None, None),
            P("tm", None),
            P(),
            P(),
            P(),
            P(),
        ),
        check_vma=False,
    )
```

profile of v0, /device:TPU:0, one launch (start us, length us, event | category | flops | bytes accessed | tf_op | source)
XLA Modules:
  0.0 163.1 jit_solution(17972851459997069887)
XLA Ops:
  7.2 0.0 all-reduce.2.cloned.1.call-start
  7.2 0.0 copy-start.2
  7.2 3.8 %convolution_bitcast_fusion.1 = f32[32,16,4,128]{3,2,1,0:T(4,128)S(1)} fusion(f32[32,16,16,128]{3,2,1,0:T(8,128)} %param.5, s32[16]{0:T(128)} %param.9), kind=kOutput, calls=%fused_computation.4 | convolution fusion | flops 50331712 | bytes 5242944 | tf_op jit(solution)/shard_map/dpsq,sr->dprq/dot_general | solution.py:48
  11.0 0.0 copy-done.2
  11.0 0.0 copy-start.1
  11.0 1.1 convolution_bitcast_fusion
  12.1 0.0 copy-start
  12.2 0.0 copy-start.3
  12.2 0.0 copy-done.1
  12.2 0.1 dynamic_slice.8
  12.3 2.5 %fusion = f32[3,32,4,128]{3,0,2,1:T(4,128)S(1)} fusion(f32[32,32,4,128]{3,1,2,0:T(8,128)S(1)} %convolution_bitcast_fusion, s32[32]{0:T(128)S(1)} %dynamic_slice.8, s32[3]{0:T(128)S(1)} %iota_add_fusion), kind=kOutput, calls=%fused_computation.1 | convolution fusion | flops 18874464 | bytes 2293900 | tf_op jit(solution)/shard_map/dcrq,dk->kcrq/dot_general | solution.py:59
  14.7 0.1 fusion.27
  14.8 1.3 collective-permute-start.1
  16.1 3.0 %collective-permute-start = (f32[1,32,4,128]{3,0,2,1:T(1,128)S(1)}, f32[1,32,4,128]{3,0,2,1:T(1,128)S(1)}, u32[]{:S(2)}, u32[]{:S(2)}) collective-permute-start(f32[1,32,4,128]{3,0,2,1:T(1,128)S(1)} %get-tuple-element.58), channel_id=1, source_target_pairs={{0,1},{1,2},{2,3},{3,4},{4,5},{5,6},{6,7},{7,8},{8,9},{9,10},{10,1... | collective-permute-start | bytes 196616 | tf_op jit(solution)/shard_map/ppermute | solution.py:16
  19.2 0.0 copy-done
  19.2 0.6 gather_fusion
  19.9 1.3 fusion.8
  21.1 0.0 all-reduce.2.cloned.1.call-update
  21.2 0.0 copy-done.3
  21.2 0.1 convert_reduce_fusion.2
  21.3 0.1 convert_reduce_fusion.1
  21.4 0.1 convert_reduce_fusion
  21.5 0.2 multiply_sqrt_fusion
  21.7 0.6 dynamic_slice.9
  22.9 0.7 maximum_sqrt_fusion.5
  23.6 0.1 maximum_sqrt_fusion.2
  23.7 0.1 maximum_sqrt_fusion.3
  23.8 0.1 maximum_sqrt_fusion
  23.8 0.1 maximum_sqrt_fusion.1
  23.9 0.1 copy.33
  24.7 0.1 copy.34
  24.8 0.1 copy.35
  24.9 0.0 collective-permute-done.1
  24.9 0.0 collective-permute-done
  24.9 0.2 fusion.25
  25.1 0.8 broadcast_divide_fusion.2
  26.0 0.7 bitcast_divide_fusion
  26.6 0.7 bitcast_divide_fusion.1
  27.3 0.5 divide_bitcast_fusion
  27.8 124.4 %all-reduce.2.cloned.1.call-done = f32[4,32,4,128]{3,0,2,1:T(4,128)} async-done(((f32[4,32,4,128]{3,0,2,1:T(4,128)}), f32[4,32,4,128]{3,0,2,1:T(4,128)}) %all-reduce.2.cloned.1.call-update) | async-done | bytes 262160 | tf_op jit(solution)/shard_map/psum | solution.py:67
  152.2 1.2 fusion.24
  153.4 0.8 copy.37
  154.1 0.1 broadcast_divide_fusion.1
  154.2 0.6 copy.38
  154.9 0.1 broadcast_divide_fusion.3
  154.9 0.6 copy.39
  155.6 0.7 broadcast_divide_fusion.4
  (5 shorter events, 0.0 us)
Async XLA Ops:
  7.2 145.0 %all-reduce.2.cloned.1.call-start = ((), (), s32[]{:S(2)}) async-start(), calls=%async_computation | async-start | bytes 524288 | tf_op jit(solution)/shard_map/psum | solution.py:67
  7.2 3.8 %copy-start.2 = (s32[16]{0:T(128)S(1)}, s32[16]{0:T(128)}, u32[]{:S(2)}) copy-start(s32[16]{0:T(128)} %param.8) | copy-start | bytes 196
  11.0 1.2 copy-start.1
  12.1 7.1 %copy-start = (s32[32]{0:T(128)S(1)}, s32[32]{0:T(128)}, u32[]{:S(2)}) copy-start(s32[32]{0:T(128)} %param.7) | copy-start | bytes 388
  12.2 9.0 %copy-start.3 = (s32[16]{0:T(128)S(1)}, s32[16]{0:T(128)}, u32[]{:S(2)}) copy-start(s32[16]{0:T(128)} %param.9) | copy-start | bytes 196
  14.8 10.1 %collective-permute-start.1 = (f32[1,32,4,128]{3,0,2,1:T(1,128)S(1)}, f32[1,32,4,128]{3,0,2,1:T(1,128)S(1)}, u32[]{:S(2)}, u32[]{:S(2)}) collective-permute-start(f32[1,32,4,128]{3,0,2,1:T(1,128)S(1)} %get-tuple-element.59), channel_id=1, source_target_pairs={{1,0},{2,1},{3,2},{4,3},{5,4},{6,5},{7,6},{8,7},{9,8},{10,9},{11,1... | collective-permute-start | bytes 196616 | tf_op jit(solution)/shard_map/ppermute | solution.py:19
  16.1 8.8 %collective-permute-start = (f32[1,32,4,128]{3,0,2,1:T(1,128)S(1)}, f32[1,32,4,128]{3,0,2,1:T(1,128)S(1)}, u32[]{:S(2)}, u32[]{:S(2)}) collective-permute-start(f32[1,32,4,128]{3,0,2,1:T(1,128)S(1)} %get-tuple-element.58), channel_id=1, source_target_pairs={{0,1},{1,2},{2,3},{3,4},{4,5},{5,6},{6,7},{7,8},{8,9},{9,10},{10,1... | collective-permute-start | bytes 196616 | tf_op jit(solution)/shard_map/ppermute | solution.py:16
Sparse Core Ops, SparseCore 0:
  21.3 130.8 all-reduce.1
where the time goes:
time: 163 us
  waiting for transfers between devices  124 us (76%)
  between operations  15.6 us (10%)
  matrix products  8.79 us (5%)
  other arithmetic  6.2 us (4%)
  starting transfers between devices  4.36 us (3%)
  local copies, waits for them, and re-layouts  3.75 us (2%)
    psum x1, waiting for transfers between devices, shards(): year_cube = lax.psum(year_part, ('tm', 'prod'))  124 us
    dot_general x1, matrix products, shards(): jnp.einsum('dpsq,sr->dprq', sales_records, region_hot, precision=highest)  3.76 us
    div x7, other arithmetic, scaled(): return sums / jnp.sqrt(counts)  3.52 us
  transfers between devices with their start and end apart: 3, of which 1 were waited for; matrix products, arithmetic and copies ran while one was open for 4% of the time, Pallas kernels for 0%

commit v1 on v0

v1 whole, which is shorter than its diff:
```python
import jax
import jax.numpy as jnp
from jax import lax
from jax.experimental import pallas as pl
from jax.experimental.pallas import tpu as pltpu
from jax.sharding import PartitionSpec as P

CATEGORY_COUNT = 32
REGION_COUNT = 4
CHUNKS = 8
VMEM = pl.BlockSpec(memory_space=pltpu.VMEM)
SMEM = pl.BlockSpec(memory_space=pltpu.SMEM)
ANY = pl.BlockSpec(memory_space=pl.ANY)


def log2(n):
    assert n & (n - 1) == 0
    return n.bit_length() - 1


def div(x, n):
    return lax.shift_right_logical(x, jnp.int32(log2(n)))


def mod(x, n):
    return lax.bitwise_and(x, jnp.int32(n - 1))


def pieces(x):
    high = x.astype(jnp.bfloat16)
    rest = x - high.astype(jnp.float32)
    mid = rest.astype(jnp.bfloat16)
    low = (rest - mid.astype(jnp.float32)).astype(jnp.bfloat16)
    return [high, mid, low]


def select_rows(hot, blocks):
    width = blocks[0].shape[1]
    out = jnp.dot(
        hot, jnp.concatenate([t for b in blocks for t in pieces(b)], axis=1), preferred_element_type=jnp.float32
    )
    cut = [out[:, i * width : (i + 1) * width] for i in range(3 * len(blocks))]
    return [(cut[3 * i + 2] + cut[3 * i + 1]) + cut[3 * i] for i in range(len(blocks))]


def local_sums(sales, day_month, month_year, store_region, year_count):
    days, products, stores, measures = sales.shape
    cells = products * REGION_COUNT
    half = year_count // 2
    step = days // CHUNKS
    months = month_year.shape[0]

    def kernel(sales_hbm, dm_hbm, my_hbm, sr_hbm, keep, send, own, far, buf, dm, my, sr, acc, sems, small):
        t = lax.axis_index("tm")
        b = lax.rem(t, 2)
        copies = [
            pltpu.make_async_copy(s, d, small.at[i])
            for i, (s, d) in enumerate(((dm_hbm, dm), (my_hbm, my), (sr_hbm, sr)))
        ]
        for c in copies:
            c.start()
        loads = [
            pltpu.make_async_copy(sales_hbm.at[pl.ds(i * step, step)], buf.at[pl.ds(i * step, step)], sems.at[i])
            for i in range(CHUNKS)
        ]
        for c in loads:
            c.start()
        for c in copies:
            c.wait()
        row = lax.broadcasted_iota(jnp.int32, (cells, products * stores), 0)
        col = lax.broadcasted_iota(jnp.int32, (cells, products * stores), 1)
        store = mod(lax.broadcasted_iota(jnp.int32, (1, products * stores), 1), stores)
        region = jnp.zeros((1, products * stores), jnp.int32)
        for s in range(stores):
            region = jnp.where(store == s, sr[s], region)
        hot = jnp.where(
            (div(row, REGION_COUNT) == div(col, stores)) & (mod(row, REGION_COUNT) == region), 1.0, 0.0
        ).astype(jnp.bfloat16)
        acc[...] = jnp.zeros_like(acc)
        for i in range(CHUNKS):
            loads[i].wait()
            side = 0 if 2 * i < CHUNKS else 2
            flags = [
                jnp.where(dm[t * days + i * step + d] == t, 1.0, 0.0).astype(jnp.float32) for d in range(step)
            ]
            for p in range(products):
                outer, inner = acc[side, p], acc[1, p]
                for d in range(step):
                    x = buf[i * step + d, p]
                    inner = inner + x * flags[d]
                    outer = outer + x * (1.0 - flags[d])
                acc[side, p], acc[1, p] = outer, inner
        sums = select_rows(hot, [acc[k].reshape(products * stores, measures) for k in range(3)])
        years = [my[jnp.clip(t - 1 + k, 0, months - 1)] for k in range(3)]
        for j in range(half):
            for ref, year in ((keep, b * half + j), (send, (1 - b) * half + j)):
                total = jnp.where(years[0] == year, sums[0], 0.0)
                total = total + jnp.where(years[1] == year, sums[1], 0.0)
                total = total + jnp.where(years[2] == year, sums[2], 0.0)
                ref[pl.ds(j * cells, cells)] = total
        send[pl.ds(half * cells, cells)] = jnp.where(b == 0, sums[2], sums[0])
        far[...] = jnp.where(b == 0, sums[0], sums[2])
        own[...] = sums[1]

    f32 = jnp.float32
    return pl.pallas_call(
        kernel,
        out_shape=[
            jax.ShapeDtypeStruct((half * cells, measures), f32),
            jax.ShapeDtypeStruct((half * cells + cells, measures), f32),
            jax.ShapeDtypeStruct((cells, measures), f32),
            jax.ShapeDtypeStruct((cells, measures), f32),
        ],
        in_specs=[ANY] * 4,
        out_specs=[VMEM] * 4,
        scratch_shapes=[
            pltpu.VMEM(sales.shape, f32),
            pltpu.SMEM(day_month.shape, jnp.int32),
            pltpu.SMEM(month_year.shape, jnp.int32),
            pltpu.SMEM(store_region.shape, jnp.int32),
            pltpu.VMEM((3, products, stores, measures), f32),
            pltpu.SemaphoreType.DMA((CHUNKS,)),
            pltpu.SemaphoreType.DMA((3,)),
        ],
        name="local_sums",
    )(sales, day_month, month_year, store_region)


def roll_up_rows(cats):
    return -(-(cats * REGION_COUNT + cats + REGION_COUNT + 1) // 8) * 8


def tables(day_month, month_year, product_category, store_region, year_count, cats, first, with_month):
    products, stores = product_category.shape[0], store_region.shape[0]
    months = month_year.shape[0]
    rows, cells = roll_up_rows(cats), products * REGION_COUNT
    a, c0, r0 = cats * REGION_COUNT, cats * REGION_COUNT + cats, cats * REGION_COUNT + cats + REGION_COUNT

    def kernel(dm, my, pc, sr, hot, factor):
        t = lax.axis_index("tm")
        base = first()

        def row_keys(shape):
            i = lax.broadcasted_iota(jnp.int32, shape, 0)
            cat = jnp.where(i < a, div(i, REGION_COUNT), jnp.where(i < c0, i - a, -1))
            reg = jnp.where(i < a, mod(i, REGION_COUNT), jnp.where((i >= c0) & (i < r0), i - c0, -1))
            return i, jnp.where(cat >= 0, cat + base, -1), reg

        i, cat, reg = row_keys((rows, cells))
        col = lax.broadcasted_iota(jnp.int32, (1, cells), 1)
        label = jnp.zeros((1, cells), jnp.int32)
        for p in range(products):
            label = jnp.where(div(col, REGION_COUNT) == p, pc[p], label)
        hit = ((cat < 0) | (cat == label)) & ((reg < 0) | (reg == mod(col, REGION_COUNT))) & (i <= r0)
        hot[...] = jnp.where(hit, 1.0, 0.0).astype(jnp.bfloat16)

        lanes = 128
        i, cat, reg = row_keys((rows, lanes))
        size = jnp.where(cat < 0, float(products), 0.0)
        for p in range(products):
            size = size + jnp.where(cat == pc[p], 1.0, 0.0)
        area = jnp.where(reg < 0, float(stores), 0.0)
        for s in range(stores):
            area = area + jnp.where(reg == sr[s], 1.0, 0.0)
        lane = lax.broadcasted_iota(jnp.int32, (1, lanes), 1)
        days = jnp.ones((1, lanes), jnp.float32)
        day = dm[...]

        def count(low, high):
            return jnp.sum(jnp.where((day >= low) & (day < high), 1.0, 0.0))

        bounds = [jnp.int32(0)] * (year_count + 1)
        for m in range(months):
            year = my[m]
            for y in range(1, year_count):
                bounds[y] = bounds[y] + jnp.where(year < y, 1, 0)
        bounds[year_count] = jnp.int32(months)
        for y in range(year_count):
            days = jnp.where(lane == y, count(bounds[y], bounds[y + 1]), days)
        days = jnp.where(lane == year_count, count(t, t + 1), days)
        cell = days * size * area
        factor[...] = 1.0 / jnp.sqrt(jnp.where(i == r0, cell, jnp.maximum(cell, 1.0)))

    return pl.pallas_call(
        kernel,
        out_shape=[
            jax.ShapeDtypeStruct((rows, cells), jnp.bfloat16),
            jax.ShapeDtypeStruct((rows, 128), jnp.float32),
        ],
        in_specs=[VMEM, SMEM, SMEM, SMEM],
        out_specs=[VMEM] * 2,
        name="tables",
    )(day_month.reshape(-1, 128), month_year, product_category, store_region)


def roll_up(hot, factor, lower, upper, months, year_count, cats):
    cells = hot.shape[1]
    measures = (lower if lower is not None else months[0]).shape[1]
    half = year_count // 2
    a, c0, r0 = cats * REGION_COUNT, cats * REGION_COUNT + cats, cats * REGION_COUNT + cats + REGION_COUNT
    years = [lower, upper]
    groups = year_count + 1

    def kernel(hot, factor, lower, upper, own, near, far, *outs):
        even = lax.rem(lax.axis_index("tm"), 2) == 0
        blocks = []
        for h in range(2):
            for j in range(half):
                x, y = lower[pl.ds(j * cells, cells)], upper[pl.ds(j * cells, cells)]
                blocks.append(jnp.where(even, x, y) if h == 0 else jnp.where(even, y, x))
        blocks.append(own[...] + near[...] + far[...])
        done = select_rows(hot[...], blocks)
        for g in range(groups):
            x = done[g] * factor[:, g : g + 1]
            refs = outs[4:] if g < year_count else outs[:4]
            at = g if g < year_count else 0
            refs[0][at] = x[:a]
            refs[1][at] = x[a:c0]
            refs[2][at] = x[c0:r0]
            refs[3][pl.ds(at, 1)] = x[r0 : r0 + 1]

    def shapes(n):
        return [
            jax.ShapeDtypeStruct((n, a, measures), jnp.float32),
            jax.ShapeDtypeStruct((n, cats, measures), jnp.float32),
            jax.ShapeDtypeStruct((n, REGION_COUNT, measures), jnp.float32),
            jax.ShapeDtypeStruct((n, measures), jnp.float32),
        ]

    outs = list(pl.pallas_call(
        kernel,
        out_shape=shapes(1) + shapes(year_count),
        in_specs=[VMEM] * 7,
        out_specs=[VMEM] * 8,
        name="roll_up",
    )(hot, factor, lower, upper, *months))
    for k, n in ((0, 1), (4, year_count)):
        outs[k] = outs[k].reshape(n, cats, REGION_COUNT, measures)
    return outs


def shards(sales_records, day_month, month_year, product_category, store_region):
    count = lax.axis_size("tm")
    year_count = max(month_year.shape[0] // 8, 2)
    cells = sales_records.shape[1] * REGION_COUNT
    half = year_count // 2 * cells

    def swap(x, distance):
        return lax.ppermute(x, "tm", [(i, i ^ distance) for i in range(count)])

    keep, send, own, far = local_sums(sales_records, day_month, month_year, store_region, year_count)
    got = swap(send, 1)
    years, near = keep + got[:half], got[half:]
    distances = [1 << k for k in range(1, log2(count))]
    if len(distances) > 1:
        distances[-2:] = distances[:-3:-1]
    edge = {0: 0, count - 1: count - 1}
    across = [(i, edge.get(i, i + 1 if i % 2 else i - 1)) for i in range(count)]
    for k, d in enumerate(distances):
        if k == len(distances) - 1:
            far, years = lax.optimization_barrier((far, years))
        years = years + swap(years, d)
        if k == len(distances) - 1:
            far = lax.ppermute(far, "tm", across)
    other = swap(years, 1)
    prods = lax.axis_size("prod")
    cats = CATEGORY_COUNT // prods
    if prods == 1:
        hot, factor = tables(
            day_month, month_year, product_category, store_region, year_count, cats, lambda: 0, True
        )
        return tuple(roll_up(hot, factor, years, other, (own, near, far), year_count, cats))

    def gathered(x):
        x = lax.all_gather(x.reshape(-1, cells, x.shape[-1]), "prod", axis=1, tiled=True)
        return x.reshape(-1, x.shape[-1])

    years, other, own, near, far = [gathered(x) for x in (years, other, own, near, far)]
    outs = []
    for n, first in ((cats, lambda: lax.axis_index("prod") * cats), (CATEGORY_COUNT, lambda: 0)):
        hot, factor = tables(day_month, month_year, product_category, store_region, year_count, n, first, True)
        outs.append(roll_up(hot, factor, years, other, (own, near, far), year_count, n))
    return tuple(outs[0][:4]) + tuple(outs[1][4:])


def solution(mesh):
    placed = (P("tm", "prod", None, None), P(), P(), P(), P())
    return jax.shard_map(
        shards,
        mesh=mesh,
        in_specs=placed,
        out_specs=(
            P("tm", "prod", None, None),
            P("tm", "prod", None),
            P("tm", None, None),
            P("tm", None),
            P(),
            P(),
            P(),
            P(),
        ),
        check_vma=False,
    )
```

time: 163 us -> 36.2 us (0.22)
  the two profiles are of different devices: /device:TPU:0 before, /device:TPU:23 now
where the time goes in v1:
time: 36.2 us; the launch traced here: 35.9 us
  waiting for transfers between devices  14.5 us (40%)
  starting transfers between devices  11.4 us (31%)
  Pallas kernels  7.14 us (20%)
  local copies, waits for them, and re-layouts  1.24 us (3%)
  other arithmetic  0.88 us (2%)
  between operations  0.68 us (2%)
    ppermute x6, waiting for transfers between devices, swap(): return lax.ppermute(x, 'tm', [(i, i ^ distance) for i in range(count)])  12.9 us
    ppermute x6, starting transfers between devices, swap(): return lax.ppermute(x, 'tm', [(i, i ^ distance) for i in range(count)])  8.3 us
    pallas_call x1, Pallas kernels, local_sums(): pl.pallas_call(kernel, out_shape=[jax.ShapeDtypeStruct((half * cells, mea...  3.22 us
    ppermute x1, starting transfers between devices, shards(): far = lax.ppermute(far, 'tm', across)  3.09 us
    pallas_call x1, Pallas kernels, roll_up(): pl.pallas_call(kernel, out_shape=shapes(1) + shapes(year_count), in_specs...  2.04 us
    pallas_call x1, Pallas kernels, tables(): pl.pallas_call(kernel, out_shape=[jax.ShapeDtypeStruct((rows, cells), jnp...  1.89 us
    ppermute x1, waiting for transfers between devices, shards(): far = lax.ppermute(far, 'tm', across)  1.64 us
    add x1, other arithmetic, shards(): years, near = (keep + got[:half], got[half:])  0.85 us
  transfers between devices with their start and end apart: 7, of which 6 were waited for; matrix products, arithmetic and copies ran while one was open for 2% of the time, Pallas kernels for 5%

profile of v1, /device:TPU:23, one launch (start us, length us, event | category | flops | bytes accessed | tf_op | source)
XLA Modules:
  0.0 35.9 jit_solution(15036635683666402624)
XLA Ops:
  0.6 3.2 %local_sums.1 = (f32[128,128]{1,0:T(8,128)}, f32[192,128]{1,0:T(8,128)}, f32[64,128]{1,0:T(8,128)}, f32[64,128]{1,0:T(8,128)}) custom-call(f32[32,16,16,128]{3,2,1,0:T(8,128)} %sales_hbm.1, s32[1024]{0:T(1024)} %dm_hbm.1, s32[32]{0:T(128)} %my_hbm.1, s32[16]{0:T(128)} %sr_hbm.1), custom_call_target="tpu_custom_call" | custom-call | tf_op jit(solution)/shard_map/local_sums/pallas_call | solution.py:106
  3.9 0.7 %collective-permute-start = (f32[192,128]{1,0:T(8,128)}, f32[192,128]{1,0:T(8,128)S(1)}, u32[]{:S(2)}, u32[]{:S(2)}) collective-permute-start(f32[192,128]{1,0:T(8,128)} %get-tuple-element.28), channel_id=1, source_target_pairs={{0,1},{1,0},{2,3},{3,2},{4,5},{5,4},{6,7},{7,6},{8,9},{9,8},{10,11... | collective-permute-start | bytes 294920 | tf_op jit(solution)/shard_map/ppermute | solution.py:249
  4.6 1.2 %collective-permute-done = f32[192,128]{1,0:T(8,128)S(1)} collective-permute-done((f32[192,128]{1,0:T(8,128)}, f32[192,128]{1,0:T(8,128)S(1)}, u32[]{:S(2)}, u32[]{:S(2)}) %collective-permute-start) | collective-permute-done | bytes 98336 | tf_op jit(solution)/shard_map/ppermute | solution.py:249
  5.8 0.8 %slice_add_fusion = f32[128,128]{1,0:T(8,128)S(1)} fusion(f32[128,128]{1,0:T(8,128)} %get-tuple-element.27, f32[192,128]{1,0:T(8,128)S(1)} %collective-permute-done), kind=kLoop, calls=%fused_computation | loop fusion | flops 16384 | bytes 196608 | tf_op jit(solution)/shard_map/add | solution.py:253
  6.6 0.3 collective-permute-start.1
  6.9 2.9 %collective-permute-done.1 = f32[128,128]{1,0:T(8,128)S(1)} collective-permute-done((f32[128,128]{1,0:T(8,128)S(1)}, f32[128,128]{1,0:T(8,128)S(1)}, u32[]{:S(2)}, u32[]{:S(2)}) %collective-permute-start.1) | collective-permute-done | bytes 65568 | tf_op jit(solution)/shard_map/ppermute | solution.py:249
  9.8 0.3 collective-permute-start.2
  10.1 2.9 %collective-permute-done.2 = f32[128,128]{1,0:T(8,128)S(1)} collective-permute-done((f32[128,128]{1,0:T(8,128)S(1)}, f32[128,128]{1,0:T(8,128)S(1)}, u32[]{:S(2)}, u32[]{:S(2)}) %collective-permute-start.2) | collective-permute-done | bytes 65568 | tf_op jit(solution)/shard_map/ppermute | solution.py:249
  13.0 0.1 collective-permute-start.3
  13.1 4.0 %collective-permute-done.3 = f32[128,128]{1,0:T(8,128)S(1)} collective-permute-done((f32[128,128]{1,0:T(8,128)S(1)}, f32[128,128]{1,0:T(8,128)S(1)}, u32[]{:S(2)}, u32[]{:S(2)}) %collective-permute-start.3) | collective-permute-done | bytes 65568 | tf_op jit(solution)/shard_map/ppermute | solution.py:249
  17.1 1.9 %collective-permute-start.4 = (f32[128,128]{1,0:T(8,128)S(1)}, f32[128,128]{1,0:T(8,128)S(1)}, u32[]{:S(2)}, u32[]{:S(2)}) collective-permute-start(f32[128,128]{1,0:T(8,128)S(1)} %add.18), channel_id=1, source_target_pairs={{0,8},{1,9},{2,10},{3,11},{4,12},{5,13},{6,14},{7,15},{8,0},{9,1},... | collective-permute-start | bytes 196616 | tf_op jit(solution)/shard_map/ppermute | solution.py:249
  19.0 2.0 %collective-permute-done.4 = f32[128,128]{1,0:T(8,128)S(1)} collective-permute-done((f32[128,128]{1,0:T(8,128)S(1)}, f32[128,128]{1,0:T(8,128)S(1)}, u32[]{:S(2)}, u32[]{:S(2)}) %collective-permute-start.4) | collective-permute-done | bytes 65568 | tf_op jit(solution)/shard_map/ppermute | solution.py:249
  21.0 0.0 copy-start
  21.0 4.9 %collective-permute-start.5 = (f32[128,128]{1,0:T(8,128)S(1)}, f32[128,128]{1,0:T(8,128)S(1)}, u32[]{:S(2)}, u32[]{:S(2)}) collective-permute-start(f32[128,128]{1,0:T(8,128)S(1)} %add.19.lower), channel_id=1, source_target_pairs={{0,1},{1,0},{2,3},{3,2},{4,5},{5,4},{6,7},{7,6},{8,9},{9,8},{10,11... | collective-permute-start | bytes 196616 | tf_op jit(solution)/shard_map/ppermute | solution.py:249
  25.9 3.1 %collective-permute-start.6 = (f32[64,128]{1,0:T(8,128)}, f32[64,128]{1,0:T(8,128)S(1)}, u32[]{:S(2)}, u32[]{:S(2)}) collective-permute-start(f32[64,128]{1,0:T(8,128)} %get-tuple-element.31), channel_id=1, source_target_pairs={{0,0},{1,2},{2,1},{3,4},{4,3},{5,6},{6,5},{7,8},{8,7},{9,10},{10,9... | collective-permute-start | bytes 98312 | tf_op jit(solution)/shard_map/ppermute | solution.py:264
  29.0 1.9 %tables.1 = (bf16[168,64]{1,0:T(8,128)(2,1)}, f32[168,128]{1,0:T(8,128)}) custom-call(s32[8,128]{1,0:T(8,128)} %bitcast.3, s32[32]{0:T(128)} %my_hbm.1, s32[16]{0:T(128)} %pc.1, s32[16]{0:T(128)} %sr_hbm.1), custom_call_target="tpu_custom_call" | custom-call | tf_op jit(solution)/shard_map/tables/pallas_call | solution.py:184
  30.9 0.6 %slice.9.near = f32[64,128]{1,0:T(8,128)} slice(f32[192,128]{1,0:T(8,128)S(1)} %collective-permute-done), slice={[128:192], [0:128]} | slice | bytes 65536 | tf_op jit(solution)/shard_map/slice | solution.py:253
  31.5 1.6 %collective-permute-done.6.far = f32[64,128]{1,0:T(8,128)S(1)} collective-permute-done((f32[64,128]{1,0:T(8,128)}, f32[64,128]{1,0:T(8,128)S(1)}, u32[]{:S(2)}, u32[]{:S(2)}) %collective-permute-start.6) | collective-permute-done | bytes 32800 | tf_op jit(solution)/shard_map/ppermute | solution.py:264
  33.2 0.0 copy-start.2
  33.2 0.0 collective-permute-done.5.upper
  33.2 0.0 copy-start.1
  33.2 0.0 copy-done
  33.2 0.6 %copy-done.2 = f32[64,128]{1,0:T(8,128)} copy-done((f32[64,128]{1,0:T(8,128)}, f32[64,128]{1,0:T(8,128)S(1)}, u32[]{:S(2)}) %copy-start.2) | copy-done | bytes 32792
  33.8 0.0 copy-done.1
  33.8 2.0 %roll_up.1 = (f32[1,128,128]{2,1,0:T(8,128)}, f32[1,32,128]{2,1,0:T(8,128)}, f32[1,4,128]{2,1,0:T(4,128)}, f32[1,128]{1,0:T(1,128)}, f32[4,128,128]{2,1,0:T(8,12...) custom-call(bf16[168,64]{1,0:T(8,128)(2,1)} %get-tuple-element.24.hot, ...), custom_call_target="tpu_custom_call" | custom-call | tf_op jit(solution)/shard_map/roll_up/pallas_call | solution.py:230
  (4 shorter events, 0.0 us)
Async XLA Ops:
  3.9 1.9 %collective-permute-start = (f32[192,128]{1,0:T(8,128)}, f32[192,128]{1,0:T(8,128)S(1)}, u32[]{:S(2)}, u32[]{:S(2)}) collective-permute-start(f32[192,128]{1,0:T(8,128)} %get-tuple-element.28), channel_id=1, source_target_pairs={{0,1},{1,0},{2,3},{3,2},{4,5},{5,4},{6,7},{7,6},{8,9},{9,8},{10,11... | collective-permute-start | bytes 294920 | tf_op jit(solution)/shard_map/ppermute | solution.py:249
  6.6 3.2 %collective-permute-start.1 = (f32[128,128]{1,0:T(8,128)S(1)}, f32[128,128]{1,0:T(8,128)S(1)}, u32[]{:S(2)}, u32[]{:S(2)}) collective-permute-start(f32[128,128]{1,0:T(8,128)S(1)} %slice_add_fusion), channel_id=1, source_target_pairs={{0,2},{1,3},{2,0},{3,1},{4,6},{5,7},{6,4},{7,5},{8,10},{9,11},{10,... | collective-permute-start | bytes 196616 | tf_op jit(solution)/shard_map/ppermute | solution.py:249
  9.8 3.2 %collective-permute-start.2 = (f32[128,128]{1,0:T(8,128)S(1)}, f32[128,128]{1,0:T(8,128)S(1)}, u32[]{:S(2)}, u32[]{:S(2)}) collective-permute-start(f32[128,128]{1,0:T(8,128)S(1)} %add.16), channel_id=1, source_target_pairs={{0,4},{1,5},{2,6},{3,7},{4,0},{5,1},{6,2},{7,3},{8,12},{9,13},{10,... | collective-permute-start | bytes 196616 | tf_op jit(solution)/shard_map/ppermute | solution.py:249
  13.0 4.1 %collective-permute-start.3 = (f32[128,128]{1,0:T(8,128)S(1)}, f32[128,128]{1,0:T(8,128)S(1)}, u32[]{:S(2)}, u32[]{:S(2)}) collective-permute-start(f32[128,128]{1,0:T(8,128)S(1)} %add.17), channel_id=1, source_target_pairs={{0,16},{1,17},{2,18},{3,19},{4,20},{5,21},{6,22},{7,23},{8,24},{9,... | collective-permute-start | bytes 196616 | tf_op jit(solution)/shard_map/ppermute | solution.py:249
  17.1 3.8 %collective-permute-start.4 = (f32[128,128]{1,0:T(8,128)S(1)}, f32[128,128]{1,0:T(8,128)S(1)}, u32[]{:S(2)}, u32[]{:S(2)}) collective-permute-start(f32[128,128]{1,0:T(8,128)S(1)} %add.18), channel_id=1, source_target_pairs={{0,8},{1,9},{2,10},{3,11},{4,12},{5,13},{6,14},{7,15},{8,0},{9,1},... | collective-permute-start | bytes 196616 | tf_op jit(solution)/shard_map/ppermute | solution.py:249
  21.0 12.2 %copy-start = (f32[128,128]{1,0:T(8,128)}, f32[128,128]{1,0:T(8,128)S(1)}, u32[]{:S(2)}) copy-start(f32[128,128]{1,0:T(8,128)S(1)} %add.19.lower) | copy-start | bytes 196612
  21.0 12.2 %collective-permute-start.5 = (f32[128,128]{1,0:T(8,128)S(1)}, f32[128,128]{1,0:T(8,128)S(1)}, u32[]{:S(2)}, u32[]{:S(2)}) collective-permute-start(f32[128,128]{1,0:T(8,128)S(1)} %add.19.lower), channel_id=1, source_target_pairs={{0,1},{1,0},{2,3},{3,2},{4,5},{5,4},{6,7},{7,6},{8,9},{9,8},{10,11... | collective-permute-start | bytes 196616 | tf_op jit(solution)/shard_map/ppermute | solution.py:249
  25.9 7.2 %collective-permute-start.6 = (f32[64,128]{1,0:T(8,128)}, f32[64,128]{1,0:T(8,128)S(1)}, u32[]{:S(2)}, u32[]{:S(2)}) collective-permute-start(f32[64,128]{1,0:T(8,128)} %get-tuple-element.31), channel_id=1, source_target_pairs={{0,0},{1,2},{2,1},{3,4},{4,3},{5,6},{6,5},{7,8},{8,7},{9,10},{10,9... | collective-permute-start | bytes 98312 | tf_op jit(solution)/shard_map/ppermute | solution.py:264
  33.2 0.6 %copy-start.2 = (f32[64,128]{1,0:T(8,128)}, f32[64,128]{1,0:T(8,128)S(1)}, u32[]{:S(2)}) copy-start(f32[64,128]{1,0:T(8,128)S(1)} %collective-permute-done.6.far) | copy-start | bytes 98308
  33.2 0.6 %copy-start.1 = (f32[128,128]{1,0:T(8,128)}, f32[128,128]{1,0:T(8,128)S(1)}, u32[]{:S(2)}) copy-start(f32[128,128]{1,0:T(8,128)S(1)} %collective-permute-done.5.upper) | copy-start | bytes 196612

commit v2 on v1

--- a/solution.py
+++ b/solution.py
@@ -106,10 +106,10 @@
     return pl.pallas_call(
         kernel,
         out_shape=[
-            jax.ShapeDtypeStruct((half * cells, measures), f32),
-            jax.ShapeDtypeStruct((half * cells + cells, measures), f32),
-            jax.ShapeDtypeStruct((cells, measures), f32),
-            jax.ShapeDtypeStruct((cells, measures), f32),
+            pltpu.VMEM((half * cells, measures), f32),
+            pltpu.VMEM((half * cells + cells, measures), f32),
+            pltpu.VMEM((cells, measures), f32),
+            pltpu.VMEM((cells, measures), f32),
         ],
         in_specs=[ANY] * 4,
         out_specs=[VMEM] * 4,
@@ -130,7 +130,7 @@
     return -(-(cats * REGION_COUNT + cats + REGION_COUNT + 1) // 8) * 8
 
 
-def tables(day_month, month_year, product_category, store_region, year_count, cats, first, with_month):
+def tables(day_month, month_year, product_category, store_region, year_count, cats, first):
     products, stores = product_category.shape[0], store_region.shape[0]
     months = month_year.shape[0]
     rows, cells = roll_up_rows(cats), products * REGION_COUNT
@@ -184,8 +184,8 @@
     return pl.pallas_call(
         kernel,
         out_shape=[
-            jax.ShapeDtypeStruct((rows, cells), jnp.bfloat16),
-            jax.ShapeDtypeStruct((rows, 128), jnp.float32),
+            pltpu.VMEM((rows, cells), jnp.bfloat16),
+            pltpu.VMEM((rows, 128), jnp.float32),
         ],
         in_specs=[VMEM, SMEM, SMEM, SMEM],
         out_specs=[VMEM] * 2,
@@ -198,7 +198,6 @@
     measures = (lower if lower is not None else months[0]).shape[1]
     half = year_count // 2
     a, c0, r0 = cats * REGION_COUNT, cats * REGION_COUNT + cats, cats * REGION_COUNT + cats + REGION_COUNT
-    years = [lower, upper]
     groups = year_count + 1
 
     def kernel(hot, factor, lower, upper, own, near, far, *outs):
@@ -233,13 +232,13 @@
         in_specs=[VMEM] * 7,
         out_specs=[VMEM] * 8,
         name="roll_up",
-    )(hot, factor, lower, upper, *months))
+    )(*[pltpu.with_memory_space_constraint(x, pltpu.VMEM) for x in (hot, factor, lower, upper, *months)]))
     for k, n in ((0, 1), (4, year_count)):
         outs[k] = outs[k].reshape(n, cats, REGION_COUNT, measures)
     return outs
 
 
-def shards(sales_records, day_month, month_year, product_category, store_region):
+def cube(sales_records, day_month, month_year, product_category, store_region):
     count = lax.axis_size("tm")
     year_count = max(month_year.shape[0] // 8, 2)
     cells = sales_records.shape[1] * REGION_COUNT
@@ -256,19 +255,20 @@
         distances[-2:] = distances[:-3:-1]
     edge = {0: 0, count - 1: count - 1}
     across = [(i, edge.get(i, i + 1 if i % 2 else i - 1)) for i in range(count)]
-    for k, d in enumerate(distances):
-        if k == len(distances) - 1:
-            far, years = lax.optimization_barrier((far, years))
-        years = years + swap(years, d)
-        if k == len(distances) - 1:
-            far = lax.ppermute(far, "tm", across)
-    other = swap(years, 1)
     prods = lax.axis_size("prod")
     cats = CATEGORY_COUNT // prods
     if prods == 1:
-        hot, factor = tables(
-            day_month, month_year, product_category, store_region, year_count, cats, lambda: 0, True
-        )
+        hot, factor = tables(day_month, month_year, product_category, store_region, year_count, cats, lambda: 0)
+    busiest = len(distances) - 2
+    for k, d in enumerate(distances):
+        if k == 1 and prods == 1:
+            years, hot, factor = lax.optimization_barrier((years, hot, factor))
+        if k == busiest:
+            far, years = lax.optimization_barrier((far, years))
+            far = lax.ppermute(far, "tm", across)
+        years = years + swap(years, d)
+    other = swap(years, 1)
+    if prods == 1:
         return tuple(roll_up(hot, factor, years, other, (own, near, far), year_count, cats))
 
     def gathered(x):
@@ -278,7 +278,7 @@
     years, other, own, near, far = [gathered(x) for x in (years, other, own, near, far)]
     outs = []
     for n, first in ((cats, lambda: lax.axis_index("prod") * cats), (CATEGORY_COUNT, lambda: 0)):
-        hot, factor = tables(day_month, month_year, product_category, store_region, year_count, n, first, True)
+        hot, factor = tables(day_month, month_year, product_category, store_region, year_count, n, first)
         outs.append(roll_up(hot, factor, years, other, (own, near, far), year_count, n))
     return tuple(outs[0][:4]) + tuple(outs[1][4:])
 
@@ -286,7 +286,7 @@
 def solution(mesh):
     placed = (P("tm", "prod", None, None), P(), P(), P(), P())
     return jax.shard_map(
-        shards,
+        cube,
         mesh=mesh,
         in_specs=placed,
         out_specs=(

time: 36.2 us -> 32.5 us (0.90)
  Pallas kernels: 7.14 us -> 4.87 us
  local copies, waits for them, and re-layouts: 1.24 us -> 0.01 us
  other arithmetic: 0.88 us -> 0.04 us
  waiting for transfers between devices: 14.5 us -> 15.3 us
    ppermute x1, waiting for transfers between devices: 1.64 us -> 3.91 us  [cube(): far = lax.ppermute(far, 'tm', across)]
    ppermute x6, waiting for transfers between devices: 12.9 us -> 11.4 us  [swap(): return lax.ppermute(x, 'tm', [(i, i ^ distance) for i in range(count)])]
    pallas_call x2, Pallas kernels: 5.11 us -> 3.79 us  [the longest x1 2.54 us: local_sums(): pl.pallas_call(kernel, out_shape=[pltpu.VMEM((half * cells, measures), f3...]
    pallas_call x1, Pallas kernels: 2.04 us -> 1.08 us  [roll_up(): pl.pallas_call(kernel, out_shape=shapes(1) + shapes(year_count), in_specs...]
    add x5, other arithmetic: 0.88 us -> 0.04 us  [the longest x4 0.04 us: cube(): years = years + swap(years, d)]
    unnamed x6 -> x0, local copies, waits for them, and re-layouts: 0.64 us -> none
    slice x1, local copies, waits for them, and re-layouts: 0.6 us -> 0.01 us  [cube(): years, near = (keep + got[:half], got[half:])]
  transfers between devices with their start and end apart: 7 -> 7, of which waited for: 6 -> 6; matrix products, arithmetic and copies ran while one was open for 2% -> 0% of each run, Pallas kernels for 5% -> 4%
where the time goes in v2:
time: 32.5 us; the launch traced here: 32.3 us
  waiting for transfers between devices  15.3 us (47%)
  starting transfers between devices  11.4 us (35%)
  Pallas kernels  4.87 us (15%)
  between operations  0.69 us (2%)
    ppermute x6, waiting for transfers between devices, swap(): return lax.ppermute(x, 'tm', [(i, i ^ distance) for i in range(count)])  11.4 us
    ppermute x6, starting transfers between devices, swap(): return lax.ppermute(x, 'tm', [(i, i ^ distance) for i in range(count)])  8.31 us
    ppermute x1, waiting for transfers between devices, cube(): far = lax.ppermute(far, 'tm', across)  3.91 us
    ppermute x1, starting transfers between devices, cube(): far = lax.ppermute(far, 'tm', across)  3.09 us
    pallas_call x1, Pallas kernels, local_sums(): pl.pallas_call(kernel, out_shape=[pltpu.VMEM((half * cells, measures), f3...  2.54 us
    pallas_call x1, Pallas kernels, tables(): pl.pallas_call(kernel, out_shape=[pltpu.VMEM((rows, cells), jnp.bfloat16)...  1.25 us
    pallas_call x1, Pallas kernels, roll_up(): pl.pallas_call(kernel, out_shape=shapes(1) + shapes(year_count), in_specs...  1.08 us
  transfers between devices with their start and end apart: 7, of which 6 were waited for; matrix products, arithmetic and copies ran while one was open for 0% of the time, Pallas kernels for 4%

profile of v2, /device:TPU:23, one launch (start us, length us, event | category | flops | bytes accessed | tf_op | source)
XLA Modules:
  0.0 32.3 jit_solution(1226474690665426428)
XLA Ops:
  0.6 2.5 %local_sums.1 = (f32[128,128]{1,0:T(8,128)S(1)}, f32[192,128]{1,0:T(8,128)S(1)}, f32[64,128]{1,0:T(8,128)S(1)}, f32[64,128]{1,0:T(8,128)S(1)}) custom-call(f32[32,16,16,128]{3,2,1,0:T(8,128)} %sales_hbm.1, s32[1024]{0:T(1024)} %dm_hbm.1, s32[32]{0:T(128)} %my.1, s32[16]{0:T(128)} %sr.1), custom_call_target="tpu_custom_call" | custom-call | tf_op jit(solution)/shard_map/local_sums/pallas_call | solution.py:106
  3.2 0.7 %collective-permute-start = (f32[192,128]{1,0:T(8,128)S(1)}, f32[192,128]{1,0:T(8,128)S(1)}, u32[]{:S(2)}, u32[]{:S(2)}) collective-permute-start(f32[192,128]{1,0:T(8,128)S(1)} %get-tuple-element.28), channel_id=1, source_target_pairs={{0,1},{1,0},{2,3},{3,2},{4,5},{5,4},{6,7},{7,6},{8,9},{9,8},{10,11... | collective-permute-start | bytes 294920 | tf_op jit(solution)/shard_map/ppermute | solution.py:248
  3.9 0.9 %collective-permute-done = f32[192,128]{1,0:T(8,128)S(1)} collective-permute-done((f32[192,128]{1,0:T(8,128)S(1)}, f32[192,128]{1,0:T(8,128)S(1)}, u32[]{:S(2)}, u32[]{:S(2)}) %collective-permute-start) | collective-permute-done | bytes 98336 | tf_op jit(solution)/shard_map/ppermute | solution.py:248
  4.9 0.3 collective-permute-start.1
  5.2 1.2 %tables.1 = (bf16[168,64]{1,0:T(8,128)(2,1)S(1)}, f32[168,128]{1,0:T(8,128)S(1)}) custom-call(s32[8,128]{1,0:T(8,128)} %bitcast.3, s32[32]{0:T(128)} %my.1, s32[16]{0:T(128)} %pc.1, s32[16]{0:T(128)} %sr.1), custom_call_target="tpu_custom_call" | custom-call | tf_op jit(solution)/shard_map/tables/pallas_call | solution.py:184
  6.5 1.6 %collective-permute-done.1 = f32[128,128]{1,0:T(8,128)S(1)} collective-permute-done((f32[128,128]{1,0:T(8,128)S(1)}, f32[128,128]{1,0:T(8,128)S(1)}, u32[]{:S(2)}, u32[]{:S(2)}) %collective-permute-start.1) | collective-permute-done | bytes 65568 | tf_op jit(solution)/shard_map/ppermute | solution.py:248
  8.1 0.3 collective-permute-start.2
  8.4 2.9 %collective-permute-done.2 = f32[128,128]{1,0:T(8,128)S(1)} collective-permute-done((f32[128,128]{1,0:T(8,128)S(1)}, f32[128,128]{1,0:T(8,128)S(1)}, u32[]{:S(2)}, u32[]{:S(2)}) %collective-permute-start.2) | collective-permute-done | bytes 65568 | tf_op jit(solution)/shard_map/ppermute | solution.py:248
  11.3 0.1 collective-permute-start.3
  11.4 4.0 %collective-permute-done.3 = f32[128,128]{1,0:T(8,128)S(1)} collective-permute-done((f32[128,128]{1,0:T(8,128)S(1)}, f32[128,128]{1,0:T(8,128)S(1)}, u32[]{:S(2)}, u32[]{:S(2)}) %collective-permute-start.3) | collective-permute-done | bytes 65568 | tf_op jit(solution)/shard_map/ppermute | solution.py:248
  15.4 1.9 %collective-permute-start.4 = (f32[128,128]{1,0:T(8,128)S(1)}, f32[128,128]{1,0:T(8,128)S(1)}, u32[]{:S(2)}, u32[]{:S(2)}) collective-permute-start(f32[128,128]{1,0:T(8,128)S(1)} %add.18), channel_id=1, source_target_pairs={{0,8},{1,9},{2,10},{3,11},{4,12},{5,13},{6,14},{7,15},{8,0},{9,1},... | collective-permute-start | bytes 196616 | tf_op jit(solution)/shard_map/ppermute | solution.py:248
  17.3 2.0 %collective-permute-done.4 = f32[128,128]{1,0:T(8,128)S(1)} collective-permute-done((f32[128,128]{1,0:T(8,128)S(1)}, f32[128,128]{1,0:T(8,128)S(1)}, u32[]{:S(2)}, u32[]{:S(2)}) %collective-permute-start.4) | collective-permute-done | bytes 65568 | tf_op jit(solution)/shard_map/ppermute | solution.py:248
  19.3 4.9 %collective-permute-start.5 = (f32[128,128]{1,0:T(8,128)S(1)}, f32[128,128]{1,0:T(8,128)S(1)}, u32[]{:S(2)}, u32[]{:S(2)}) collective-permute-start(f32[128,128]{1,0:T(8,128)S(1)} %add.19.lower), channel_id=1, source_target_pairs={{0,1},{1,0},{2,3},{3,2},{4,5},{5,4},{6,7},{7,6},{8,9},{9,8},{10,11... | collective-permute-start | bytes 196616 | tf_op jit(solution)/shard_map/ppermute | solution.py:248
  24.2 3.1 %collective-permute-start.6 = (f32[64,128]{1,0:T(8,128)S(1)}, f32[64,128]{1,0:T(8,128)S(1)}, u32[]{:S(2)}, u32[]{:S(2)}) collective-permute-start(f32[64,128]{1,0:T(8,128)S(1)} %get-tuple-element.37), channel_id=1, source_target_pairs={{0,0},{1,2},{2,1},{3,4},{4,3},{5,6},{6,5},{7,8},{8,7},{9,10},{10,9... | collective-permute-start | bytes 98312 | tf_op jit(solution)/shard_map/ppermute | solution.py:268
  27.3 3.9 %collective-permute-done.6.far = f32[64,128]{1,0:T(8,128)S(1)} collective-permute-done((f32[64,128]{1,0:T(8,128)S(1)}, f32[64,128]{1,0:T(8,128)S(1)}, u32[]{:S(2)}, u32[]{:S(2)}) %collective-permute-start.6) | collective-permute-done | bytes 32800 | tf_op jit(solution)/shard_map/ppermute | solution.py:268
  31.2 0.0 collective-permute-done.5.upper
  31.2 1.1 %roll_up.1 = (f32[1,128,128]{2,1,0:T(8,128)}, f32[1,32,128]{2,1,0:T(8,128)}, f32[1,4,128]{2,1,0:T(4,128)}, f32[1,128]{1,0:T(1,128)}, f32[4,128,128]{2,1,0:T(8,12...) custom-call(bf16[168,64]{1,0:T(8,128)(2,1)S(1)} %get-tuple-element.31.hot, ...), custom_call_target="tpu_custom_call" | custom-call | tf_op jit(solution)/shard_map/roll_up/pallas_call | solution.py:229
  (6 shorter events, 0.0 us)
Async XLA Ops:
  3.2 1.7 %collective-permute-start = (f32[192,128]{1,0:T(8,128)S(1)}, f32[192,128]{1,0:T(8,128)S(1)}, u32[]{:S(2)}, u32[]{:S(2)}) collective-permute-start(f32[192,128]{1,0:T(8,128)S(1)} %get-tuple-element.28), channel_id=1, source_target_pairs={{0,1},{1,0},{2,3},{3,2},{4,5},{5,4},{6,7},{7,6},{8,9},{9,8},{10,11... | collective-permute-start | bytes 294920 | tf_op jit(solution)/shard_map/ppermute | solution.py:248
  4.9 3.2 %collective-permute-start.1 = (f32[128,128]{1,0:T(8,128)S(1)}, f32[128,128]{1,0:T(8,128)S(1)}, u32[]{:S(2)}, u32[]{:S(2)}) collective-permute-start(f32[128,128]{1,0:T(8,128)S(1)} %slice_add_fusion), channel_id=1, source_target_pairs={{0,2},{1,3},{2,0},{3,1},{4,6},{5,7},{6,4},{7,5},{8,10},{9,11},{10,... | collective-permute-start | bytes 196616 | tf_op jit(solution)/shard_map/ppermute | solution.py:248
  8.1 3.2 %collective-permute-start.2 = (f32[128,128]{1,0:T(8,128)S(1)}, f32[128,128]{1,0:T(8,128)S(1)}, u32[]{:S(2)}, u32[]{:S(2)}) collective-permute-start(f32[128,128]{1,0:T(8,128)S(1)} %add.16), channel_id=1, source_target_pairs={{0,4},{1,5},{2,6},{3,7},{4,0},{5,1},{6,2},{7,3},{8,12},{9,13},{10,... | collective-permute-start | bytes 196616 | tf_op jit(solution)/shard_map/ppermute | solution.py:248
  11.3 4.1 %collective-permute-start.3 = (f32[128,128]{1,0:T(8,128)S(1)}, f32[128,128]{1,0:T(8,128)S(1)}, u32[]{:S(2)}, u32[]{:S(2)}) collective-permute-start(f32[128,128]{1,0:T(8,128)S(1)} %add.17), channel_id=1, source_target_pairs={{0,16},{1,17},{2,18},{3,19},{4,20},{5,21},{6,22},{7,23},{8,24},{9,... | collective-permute-start | bytes 196616 | tf_op jit(solution)/shard_map/ppermute | solution.py:248
  15.4 3.8 %collective-permute-start.4 = (f32[128,128]{1,0:T(8,128)S(1)}, f32[128,128]{1,0:T(8,128)S(1)}, u32[]{:S(2)}, u32[]{:S(2)}) collective-permute-start(f32[128,128]{1,0:T(8,128)S(1)} %add.18), channel_id=1, source_target_pairs={{0,8},{1,9},{2,10},{3,11},{4,12},{5,13},{6,14},{7,15},{8,0},{9,1},... | collective-permute-start | bytes 196616 | tf_op jit(solution)/shard_map/ppermute | solution.py:248
  19.3 12.0 %collective-permute-start.5 = (f32[128,128]{1,0:T(8,128)S(1)}, f32[128,128]{1,0:T(8,128)S(1)}, u32[]{:S(2)}, u32[]{:S(2)}) collective-permute-start(f32[128,128]{1,0:T(8,128)S(1)} %add.19.lower), channel_id=1, source_target_pairs={{0,1},{1,0},{2,3},{3,2},{4,5},{5,4},{6,7},{7,6},{8,9},{9,8},{10,11... | collective-permute-start | bytes 196616 | tf_op jit(solution)/shard_map/ppermute | solution.py:248
  24.2 7.0 %collective-permute-start.6 = (f32[64,128]{1,0:T(8,128)S(1)}, f32[64,128]{1,0:T(8,128)S(1)}, u32[]{:S(2)}, u32[]{:S(2)}) collective-permute-start(f32[64,128]{1,0:T(8,128)S(1)} %get-tuple-element.37), channel_id=1, source_target_pairs={{0,0},{1,2},{2,1},{3,4},{4,3},{5,6},{6,5},{7,8},{8,7},{9,10},{10,9... | collective-permute-start | bytes 98312 | tf_op jit(solution)/shard_map/ppermute | solution.py:268

commit v3 on v2

--- a/solution.py
+++ b/solution.py
@@ -11,6 +11,16 @@
 VMEM = pl.BlockSpec(memory_space=pltpu.VMEM)
 SMEM = pl.BlockSpec(memory_space=pltpu.SMEM)
 ANY = pl.BlockSpec(memory_space=pl.ANY)
+
+
+def rounds_of(count):
+    bits = [1 << k for k in range(1, log2(count))]
+    rounds = []
+    while bits:
+        pair = bits[:: max(len(bits) // 2, 1)][:2]
+        bits = [b for b in bits if b not in pair]
+        rounds.append(tuple((pair[0] + pair[1], pair[1], pair[0])) if len(pair) > 1 else tuple(pair))
+    return rounds
 
 
 def log2(n):
@@ -250,23 +260,23 @@
     keep, send, own, far = local_sums(sales_records, day_month, month_year, store_region, year_count)
     got = swap(send, 1)
     years, near = keep + got[:half], got[half:]
-    distances = [1 << k for k in range(1, log2(count))]
-    if len(distances) > 1:
-        distances[-2:] = distances[:-3:-1]
+    rounds = rounds_of(count)
     edge = {0: 0, count - 1: count - 1}
     across = [(i, edge.get(i, i + 1 if i % 2 else i - 1)) for i in range(count)]
     prods = lax.axis_size("prod")
     cats = CATEGORY_COUNT // prods
     if prods == 1:
         hot, factor = tables(day_month, month_year, product_category, store_region, year_count, cats, lambda: 0)
-    busiest = len(distances) - 2
-    for k, d in enumerate(distances):
+    for k, distances in enumerate(rounds):
         if k == 1 and prods == 1:
             years, hot, factor = lax.optimization_barrier((years, hot, factor))
-        if k == busiest:
+        if k == len(rounds) - 1:
             far, years = lax.optimization_barrier((far, years))
             far = lax.ppermute(far, "tm", across)
-        years = years + swap(years, d)
+        total = years
+        for d in distances:
+            total = total + swap(years, d)
+        years = total
     other = swap(years, 1)
     if prods == 1:
         return tuple(roll_up(hot, factor, years, other, (own, near, far), year_count, cats))

time: 32.5 us -> 31.8 us (0.978)
  the two profiles are of different devices: /device:TPU:23 before, /device:TPU:1 now
where the time goes in v3:
time: 31.8 us; the launch traced here: 31.6 us
  waiting for transfers between devices  13.6 us (43%)
  starting transfers between devices  12.5 us (39%)
  Pallas kernels  4.87 us (15%)
  between operations  0.69 us (2%)
    ppermute x8, waiting for transfers between devices, swap(): return lax.ppermute(x, 'tm', [(i, i ^ distance) for i in range(count)])  10.5 us
    ppermute x8, starting transfers between devices, swap(): return lax.ppermute(x, 'tm', [(i, i ^ distance) for i in range(count)])  10.3 us
    ppermute x1, waiting for transfers between devices, cube(): far = lax.ppermute(far, 'tm', across)  3.05 us
    pallas_call x1, Pallas kernels, local_sums(): pl.pallas_call(kernel, out_shape=[pltpu.VMEM((half * cells, measures), f3...  2.54 us
    ppermute x1, starting transfers between devices, cube(): far = lax.ppermute(far, 'tm', across)  2.15 us
    pallas_call x1, Pallas kernels, tables(): pl.pallas_call(kernel, out_shape=[pltpu.VMEM((rows, cells), jnp.bfloat16)...  1.25 us
    pallas_call x1, Pallas kernels, roll_up(): pl.pallas_call(kernel, out_shape=shapes(1) + shapes(year_count), in_specs...  1.08 us
  transfers between devices with their start and end apart: 9, of which 6 were waited for; matrix products, arithmetic and copies ran while one was open for 0% of the time, Pallas kernels for 4%

profile of v3, /device:TPU:1, one launch (start us, length us, event | category | flops | bytes accessed | tf_op | source)
XLA Modules:
  0.0 31.6 jit_solution(7942129428194486594)
XLA Ops:
  0.6 2.5 %local_sums.1 = (f32[128,128]{1,0:T(8,128)S(1)}, f32[192,128]{1,0:T(8,128)S(1)}, f32[64,128]{1,0:T(8,128)S(1)}, f32[64,128]{1,0:T(8,128)S(1)}) custom-call(f32[32,16,16,128]{3,2,1,0:T(8,128)} %sales_hbm.1, s32[1024]{0:T(1024)} %dm_hbm.1, s32[32]{0:T(128)} %my.1, s32[16]{0:T(128)} %sr.1), custom_call_target="tpu_custom_call" | custom-call | tf_op jit(solution)/shard_map/local_sums/pallas_call | solution.py:116
  3.2 0.1 collective-permute-start
  3.3 1.3 %collective-permute-done = f32[192,128]{1,0:T(8,128)S(1)} collective-permute-done((f32[192,128]{1,0:T(8,128)S(1)}, f32[192,128]{1,0:T(8,128)S(1)}, u32[]{:S(2)}, u32[]{:S(2)}) %collective-permute-start) | collective-permute-done | bytes 98336 | tf_op jit(solution)/shard_map/ppermute | solution.py:258
  4.6 2.4 %collective-permute-start.3 = (f32[128,128]{1,0:T(8,128)S(1)}, f32[128,128]{1,0:T(8,128)S(1)}, u32[]{:S(2)}, u32[]{:S(2)}) collective-permute-start(f32[128,128]{1,0:T(8,128)S(1)} %slice_add_fusion), channel_id=1, source_target_pairs={{0,2},{1,3},{2,0},{3,1},{4,6},{5,7},{6,4},{7,5},{8,10},{9,11},{10,... | collective-permute-start | bytes 196616 | tf_op jit(solution)/shard_map/ppermute | solution.py:258
  7.0 1.3 %collective-permute-start.2 = (f32[128,128]{1,0:T(8,128)S(1)}, f32[128,128]{1,0:T(8,128)S(1)}, u32[]{:S(2)}, u32[]{:S(2)}) collective-permute-start(f32[128,128]{1,0:T(8,128)S(1)} %slice_add_fusion), channel_id=1, source_target_pairs={{0,8},{1,9},{2,10},{3,11},{4,12},{5,13},{6,14},{7,15},{8,0},{9,1},... | collective-permute-start | bytes 196616 | tf_op jit(solution)/shard_map/ppermute | solution.py:258
  8.3 0.0 collective-permute-start.1
  8.3 1.3 %tables.1 = (bf16[168,64]{1,0:T(8,128)(2,1)S(1)}, f32[168,128]{1,0:T(8,128)S(1)}) custom-call(s32[8,128]{1,0:T(8,128)} %bitcast.3, s32[32]{0:T(128)} %my.1, s32[16]{0:T(128)} %pc.1, s32[16]{0:T(128)} %sr.1), custom_call_target="tpu_custom_call" | custom-call | tf_op jit(solution)/shard_map/tables/pallas_call | solution.py:194
  9.5 0.0 collective-permute-done.3
  9.5 0.5 %collective-permute-done.2 = f32[128,128]{1,0:T(8,128)S(1)} collective-permute-done((f32[128,128]{1,0:T(8,128)S(1)}, f32[128,128]{1,0:T(8,128)S(1)}, u32[]{:S(2)}, u32[]{:S(2)}) %collective-permute-start.2) | collective-permute-done | bytes 65568 | tf_op jit(solution)/shard_map/ppermute | solution.py:258
  10.1 2.2 %collective-permute-done.1 = f32[128,128]{1,0:T(8,128)S(1)} collective-permute-done((f32[128,128]{1,0:T(8,128)S(1)}, f32[128,128]{1,0:T(8,128)S(1)}, u32[]{:S(2)}, u32[]{:S(2)}) %collective-permute-start.1) | collective-permute-done | bytes 65568 | tf_op jit(solution)/shard_map/ppermute | solution.py:258
  12.3 1.3 %collective-permute-start.6 = (f32[128,128]{1,0:T(8,128)S(1)}, f32[128,128]{1,0:T(8,128)S(1)}, u32[]{:S(2)}, u32[]{:S(2)}) collective-permute-start(f32[128,128]{1,0:T(8,128)S(1)} %add_add_fusion.1), channel_id=1, source_target_pairs={{0,4},{1,5},{2,6},{3,7},{4,0},{5,1},{6,2},{7,3},{8,12},{9,13},{10,... | collective-permute-start | bytes 196616 | tf_op jit(solution)/shard_map/ppermute | solution.py:258
  13.6 2.3 %collective-permute-start.5 = (f32[128,128]{1,0:T(8,128)S(1)}, f32[128,128]{1,0:T(8,128)S(1)}, u32[]{:S(2)}, u32[]{:S(2)}) collective-permute-start(f32[128,128]{1,0:T(8,128)S(1)} %add_add_fusion.1), channel_id=1, source_target_pairs={{0,16},{1,17},{2,18},{3,19},{4,20},{5,21},{6,22},{7,23},{8,24},{9,... | collective-permute-start | bytes 196616 | tf_op jit(solution)/shard_map/ppermute | solution.py:258
  15.9 0.0 collective-permute-start.4
  15.9 0.0 collective-permute-done.6
  15.9 2.4 %collective-permute-done.5 = f32[128,128]{1,0:T(8,128)S(1)} collective-permute-done((f32[128,128]{1,0:T(8,128)S(1)}, f32[128,128]{1,0:T(8,128)S(1)}, u32[]{:S(2)}, u32[]{:S(2)}) %collective-permute-start.5) | collective-permute-done | bytes 65568 | tf_op jit(solution)/shard_map/ppermute | solution.py:258
  18.3 4.1 %collective-permute-done.4 = f32[128,128]{1,0:T(8,128)S(1)} collective-permute-done((f32[128,128]{1,0:T(8,128)S(1)}, f32[128,128]{1,0:T(8,128)S(1)}, u32[]{:S(2)}, u32[]{:S(2)}) %collective-permute-start.4) | collective-permute-done | bytes 65568 | tf_op jit(solution)/shard_map/ppermute | solution.py:258
  22.4 2.9 %collective-permute-start.7 = (f32[128,128]{1,0:T(8,128)S(1)}, f32[128,128]{1,0:T(8,128)S(1)}, u32[]{:S(2)}, u32[]{:S(2)}) collective-permute-start(f32[128,128]{1,0:T(8,128)S(1)} %add_add_fusion.lower), channel_id=1, source_target_pairs={{0,1},{1,0},{2,3},{3,2},{4,5},{5,4},{6,7},{7,6},{8,9},{9,8},{10,11... | collective-permute-start | bytes 196616 | tf_op jit(solution)/shard_map/ppermute | solution.py:258
  25.3 2.1 %collective-permute-start.8 = (f32[64,128]{1,0:T(8,128)S(1)}, f32[64,128]{1,0:T(8,128)S(1)}, u32[]{:S(2)}, u32[]{:S(2)}) collective-permute-start(f32[64,128]{1,0:T(8,128)S(1)} %get-tuple-element.37), channel_id=1, source_target_pairs={{0,0},{1,2},{2,1},{3,4},{4,3},{5,6},{6,5},{7,8},{8,7},{9,10},{10,9... | collective-permute-start | bytes 98312 | tf_op jit(solution)/shard_map/ppermute | solution.py:275
  27.5 3.1 %collective-permute-done.8.far = f32[64,128]{1,0:T(8,128)S(1)} collective-permute-done((f32[64,128]{1,0:T(8,128)S(1)}, f32[64,128]{1,0:T(8,128)S(1)}, u32[]{:S(2)}, u32[]{:S(2)}) %collective-permute-start.8) | collective-permute-done | bytes 32800 | tf_op jit(solution)/shard_map/ppermute | solution.py:275
  30.5 0.0 collective-permute-done.7.upper
  30.5 1.1 %roll_up.1 = (f32[1,128,128]{2,1,0:T(8,128)}, f32[1,32,128]{2,1,0:T(8,128)}, f32[1,4,128]{2,1,0:T(4,128)}, f32[1,128]{1,0:T(1,128)}, f32[4,128,128]{2,1,0:T(8,12...) custom-call(bf16[168,64]{1,0:T(8,128)(2,1)S(1)} %get-tuple-element.31.hot, ...), custom_call_target="tpu_custom_call" | custom-call | tf_op jit(solution)/shard_map/roll_up/pallas_call | solution.py:239
  (4 shorter events, 0.0 us)
Async XLA Ops:
  3.2 1.4 %collective-permute-start = (f32[192,128]{1,0:T(8,128)S(1)}, f32[192,128]{1,0:T(8,128)S(1)}, u32[]{:S(2)}, u32[]{:S(2)}) collective-permute-start(f32[192,128]{1,0:T(8,128)S(1)} %get-tuple-element.28), channel_id=1, source_target_pairs={{0,1},{1,0},{2,3},{3,2},{4,5},{5,4},{6,7},{7,6},{8,9},{9,8},{10,11... | collective-permute-start | bytes 294920 | tf_op jit(solution)/shard_map/ppermute | solution.py:258
  4.6 5.0 %collective-permute-start.3 = (f32[128,128]{1,0:T(8,128)S(1)}, f32[128,128]{1,0:T(8,128)S(1)}, u32[]{:S(2)}, u32[]{:S(2)}) collective-permute-start(f32[128,128]{1,0:T(8,128)S(1)} %slice_add_fusion), channel_id=1, source_target_pairs={{0,2},{1,3},{2,0},{3,1},{4,6},{5,7},{6,4},{7,5},{8,10},{9,11},{10,... | collective-permute-start | bytes 196616 | tf_op jit(solution)/shard_map/ppermute | solution.py:258
  7.0 3.1 %collective-permute-start.2 = (f32[128,128]{1,0:T(8,128)S(1)}, f32[128,128]{1,0:T(8,128)S(1)}, u32[]{:S(2)}, u32[]{:S(2)}) collective-permute-start(f32[128,128]{1,0:T(8,128)S(1)} %slice_add_fusion), channel_id=1, source_target_pairs={{0,8},{1,9},{2,10},{3,11},{4,12},{5,13},{6,14},{7,15},{8,0},{9,1},... | collective-permute-start | bytes 196616 | tf_op jit(solution)/shard_map/ppermute | solution.py:258
  8.3 4.0 %collective-permute-start.1 = (f32[128,128]{1,0:T(8,128)S(1)}, f32[128,128]{1,0:T(8,128)S(1)}, u32[]{:S(2)}, u32[]{:S(2)}) collective-permute-start(f32[128,128]{1,0:T(8,128)S(1)} %slice_add_fusion), channel_id=1, source_target_pairs={{0,10},{1,11},{2,8},{3,9},{4,14},{5,15},{6,12},{7,13},{8,2},{9,3},... | collective-permute-start | bytes 196616 | tf_op jit(solution)/shard_map/ppermute | solution.py:258
  12.3 3.6 %collective-permute-start.6 = (f32[128,128]{1,0:T(8,128)S(1)}, f32[128,128]{1,0:T(8,128)S(1)}, u32[]{:S(2)}, u32[]{:S(2)}) collective-permute-start(f32[128,128]{1,0:T(8,128)S(1)} %add_add_fusion.1), channel_id=1, source_target_pairs={{0,4},{1,5},{2,6},{3,7},{4,0},{5,1},{6,2},{7,3},{8,12},{9,13},{10,... | collective-permute-start | bytes 196616 | tf_op jit(solution)/shard_map/ppermute | solution.py:258
  13.6 4.7 %collective-permute-start.5 = (f32[128,128]{1,0:T(8,128)S(1)}, f32[128,128]{1,0:T(8,128)S(1)}, u32[]{:S(2)}, u32[]{:S(2)}) collective-permute-start(f32[128,128]{1,0:T(8,128)S(1)} %add_add_fusion.1), channel_id=1, source_target_pairs={{0,16},{1,17},{2,18},{3,19},{4,20},{5,21},{6,22},{7,23},{8,24},{9,... | collective-permute-start | bytes 196616 | tf_op jit(solution)/shard_map/ppermute | solution.py:258
  15.9 6.5 %collective-permute-start.4 = (f32[128,128]{1,0:T(8,128)S(1)}, f32[128,128]{1,0:T(8,128)S(1)}, u32[]{:S(2)}, u32[]{:S(2)}) collective-permute-start(f32[128,128]{1,0:T(8,128)S(1)} %add_add_fusion.1), channel_id=1, source_target_pairs={{0,20},{1,21},{2,22},{3,23},{4,16},{5,17},{6,18},{7,19},{8,28},{9,... | collective-permute-start | bytes 196616 | tf_op jit(solution)/shard_map/ppermute | solution.py:258
  22.4 8.1 %collective-permute-start.7 = (f32[128,128]{1,0:T(8,128)S(1)}, f32[128,128]{1,0:T(8,128)S(1)}, u32[]{:S(2)}, u32[]{:S(2)}) collective-permute-start(f32[128,128]{1,0:T(8,128)S(1)} %add_add_fusion.lower), channel_id=1, source_target_pairs={{0,1},{1,0},{2,3},{3,2},{4,5},{5,4},{6,7},{7,6},{8,9},{9,8},{10,11... | collective-permute-start | bytes 196616 | tf_op jit(solution)/shard_map/ppermute | solution.py:258
  25.3 5.2 %collective-permute-start.8 = (f32[64,128]{1,0:T(8,128)S(1)}, f32[64,128]{1,0:T(8,128)S(1)}, u32[]{:S(2)}, u32[]{:S(2)}) collective-permute-start(f32[64,128]{1,0:T(8,128)S(1)} %get-tuple-element.37), channel_id=1, source_target_pairs={{0,0},{1,2},{2,1},{3,4},{4,3},{5,6},{6,5},{7,8},{8,7},{9,10},{10,9... | collective-permute-start | bytes 98312 | tf_op jit(solution)/shard_map/ppermute | solution.py:275
